TPU v7x, 128 devices: a whole 4x4x4 slice. The times are simulated.
128 devices in a mesh: fsdp: 64 (over z, y, x), ep: 2 (over core).
Axes of the slice: x: 4, y: 4, z: 4, core: 2. Of those that a mesh axis runs over, the one named last changes fastest.
Arguments:
- x_in: bfloat16 [2, 131072, 512], P(None, ('fsdp', 'ep'))
- dy_out: bfloat16 [2, 131072, 512], P(None, ('fsdp', 'ep'))
- expert_idx: int32 [2, 131072, 2], P(None, ('fsdp', 'ep'))
- gate_prob: float32 [2, 131072, 2], P(None, ('fsdp', 'ep'))
- w_one: bfloat16 [8, 512, 1792], P('ep', 'fsdp')
- w_two: bfloat16 [8, 1792, 512], P('ep', None, 'fsdp')
- w_three: bfloat16 [8, 512, 1792], P('ep', 'fsdp')
Outputs:
- output 1: bfloat16 [2, 131072, 512], P(None, ('fsdp', 'ep'))
- output 2: float32 [2, 131072, 2], P(None, ('fsdp', 'ep'))
- output 3: float32 [8, 512, 1792], P('ep', 'fsdp')
- output 4: float32 [8, 1792, 512], P('ep', None, 'fsdp')
- output 5: float32 [8, 512, 1792], P('ep', 'fsdp')
All inputs are finite; a program needn't handle non-finite values.
Results may differ from a plain program's by a relative error of at most 0.00102.
Values are sent between devices in bfloat16 or wider.
A program may use at most 1 GiB of HBM per device.

v0:
```python
import functools

import jax
import jax.numpy as jnp
from jax import lax
from jax.experimental import pallas as pl
from jax.experimental.pallas import tpu as pltpu
from jax.sharding import Mesh, PartitionSpec as P


F32 = jnp.float32
BF16 = jnp.bfloat16
UNIT = 16
COL_TILE = 256
NT_DIMS = (((1,),(1,)),((),()))


def row_pieces(n_sm, cap, emit):
    off = jnp.int32(0)
    for s in range(n_sm.shape[0]):
        n = n_sm[s]
        for k in range(cap // 64):
            @pl.when((k + 1) * 4 <= n)
            def _(k=k, s=s, off=off):
                emit(s * cap + k * 64, off * UNIT + k * 64, 64)
        base = (n // 4) * 4

        @pl.when((n // 2) % 2 == 1)
        def _(s=s, off=off, base=base):
            emit(s * cap + base * UNIT, (off + base) * UNIT, 32)

        tail = (n // 2) * 2

        @pl.when(n % 2 == 1)
        def _(s=s, off=off, tail=tail):
            emit(s * cap + tail * UNIT, (off + tail) * UNIT, 16)

        off = off + n
    return off


def expert_kernel(ff, cap, first, n_sm, xdy_hbm, q_ref, w_hbm, *rest):
    if first:
        dx_hbm, dg_ref, gw_hbm, xdy_v, q_v, dg_v, dx_v, w_v, gw_v, xt_v, gt_v, sems = rest
        gin_hbm = gin_v = None
    else:
        gin_hbm, dx_hbm, dg_ref, gw_hbm, xdy_v, q_v, dg_v, dx_v, w_v, gw_v, xt_v, gt_v, gin_v, sems = rest
    d = w_hbm.shape[0]
    n_src = n_sm.shape[0]

    def m8(v, n=UNIT):
        return v if isinstance(v, int) else pl.multiple_of(v, n)

    def fetch(slot, packed, size):
        return pltpu.make_async_copy(xdy_hbm.at[pl.ds(m8(slot), size)], xdy_v.at[pl.ds(m8(packed), size)], sems.at[0])

    units = row_pieces(n_sm, cap, lambda *a: fetch(*a).start())
    parts = [pltpu.make_async_copy(w_hbm.at[:, pl.ds(k * ff, ff)], w_v.at[:, pl.ds(k * ff, ff)], sems.at[1 + k]) for k in range(3)]
    for p in parts:
        p.start()
    if not first:
        gin = pltpu.make_async_copy(gin_hbm, gin_v, sems.at[4])
        gin.start()
    gw_v[...] = jnp.zeros_like(gw_v)
    q_cols = q_ref[...].T
    off = jnp.int32(0)
    for s in range(n_src):
        q_v[pl.ds(pl.multiple_of(off * UNIT, UNIT), cap), :] = q_cols[:, s:s + 1]
        off = off + n_sm[s]
    q_v[pl.ds(pl.multiple_of(off * UNIT, UNIT), 512), :] = jnp.zeros((512, 1), F32)

    def clear(i, c):
        xdy_v[pl.ds(pl.multiple_of(i * UNIT, UNIT), UNIT), :] = jnp.zeros((UNIT, 2 * d), BF16)
        return c

    lax.fori_loop(units, ((units + 31) // 32) * 32, clear, 0)
    row_pieces(n_sm, cap, lambda *a: fetch(*a).wait())
    for p in parts:
        p.wait()

    dot = functools.partial(jnp.dot, preferred_element_type=F32)
    dot_nt = lambda a, b: lax.dot_general(a, b, NT_DIMS, preferred_element_type=F32)

    def tile(lo_row, rt):
        rows = pl.ds(pl.multiple_of(lo_row, 256), rt)
        x = xdy_v[rows, :d]
        dy = xdy_v[rows, d:]
        g = (q_v[rows, :] * dy.astype(F32)).astype(BF16)
        xt_v[:, :rt] = x.T
        gt_v[:, :rt] = g.T
        y = None
        dx = None
        for lo in range(0, ff, COL_TILE):
            one, two, three = (pl.ds(k * ff + lo, COL_TILE) for k in range(3))
            h_one = dot(x, w_v[:, one])
            h_three = dot(x, w_v[:, three])
            d_act = dot(g, w_v[:, two])
            sigma = jax.nn.sigmoid(h_one)
            silu = h_one * sigma
            act = (silu * h_three).astype(BF16)
            dh_three = (d_act * silu).astype(BF16)
            dh_one = (d_act * h_three * sigma * (1.0 + h_one * (1.0 - sigma))).astype(BF16)
            y_part = dot_nt(act, w_v[:, two])
            dx_part = dot_nt(dh_one, w_v[:, one]) + dot_nt(dh_three, w_v[:, three])
            y = y_part if y is None else y + y_part
            dx = dx_part if dx is None else dx + dx_part
            gw_v[:, one] += dot(xt_v[:, :rt], dh_one)
            gw_v[:, three] += dot(xt_v[:, :rt], dh_three)
            gw_v[:, two] += dot(gt_v[:, :rt], act)
        dg_v[rows, :] = jnp.sum(dy.astype(F32) * y, axis=1, keepdims=True)
        dx_v[rows, :] = dx.astype(BF16)

    total = units * UNIT
    full = (total + 511) // 512

    def big(i, c):
        tile(i * 512, 512)
        return c

    lax.fori_loop(0, full, big, 0)

    if not first:
        gin.wait()
    outs = []
    for k in range(3):
        cols = pl.ds(k * ff, ff)
        if not first:
            gw_v[:, cols] += gin_v[:, cols]
        o = pltpu.make_async_copy(gw_v.at[:, cols], gw_hbm.at[:, cols], sems.at[1 + k])
        o.start()
        outs.append(o)

    def put(slot, packed, size):
        return pltpu.make_async_copy(dx_v.at[pl.ds(m8(packed), size)], dx_hbm.at[pl.ds(m8(slot), size)], sems.at[0])

    row_pieces(n_sm, cap, lambda *a: put(*a).start())
    off = jnp.int32(0)
    cols = []
    for s in range(n_src):
        cols.append(dg_v[pl.ds(pl.multiple_of(off * UNIT, UNIT), cap), :])
        off = off + n_sm[s]
    dg_ref[...] = jnp.concatenate(cols, axis=1).T
    row_pieces(n_sm, cap, lambda *a: put(*a).wait())
    for o in outs:
        o.wait()


def expert_pass(n_units, xdy, gates, w_full, grad_in):
    rows, d2 = xdy.shape
    d = d2 // 2
    ff = w_full.shape[1] // 3
    cap = gates.shape[1]
    first = grad_in is None
    whole = pl.BlockSpec(memory_space=pl.ANY)
    vm = pl.BlockSpec(memory_space=pltpu.VMEM)
    args = [n_units, xdy, gates, w_full] + ([] if first else [grad_in])
    in_specs = [pl.BlockSpec(memory_space=pltpu.SMEM), whole, vm, whole] + ([] if first else [whole])
    pad = rows + 512
    scratch = [
        pltpu.VMEM((rows, d2), BF16), pltpu.VMEM((pad, 1), F32), pltpu.VMEM((pad, 1), F32), pltpu.VMEM((rows, d), BF16),
        pltpu.VMEM((d, 3 * ff), BF16), pltpu.VMEM((d, 3 * ff), F32), pltpu.VMEM((d, 512), BF16), pltpu.VMEM((d, 512), BF16)]
    if not first:
        scratch.append(pltpu.VMEM((d, 3 * ff), F32))
    scratch.append(pltpu.SemaphoreType.DMA((5,)))
    return pl.pallas_call(
        functools.partial(expert_kernel, ff, cap, first),
        in_specs=in_specs, out_specs=[whole, vm, whole],
        out_shape=[jax.ShapeDtypeStruct((rows, d), BF16), jax.ShapeDtypeStruct(gates.shape, F32), jax.ShapeDtypeStruct((d, 3 * ff), F32)],
        scratch_shapes=scratch,
        compiler_params=pltpu.CompilerParams(vmem_limit_bytes=60 * 2**20),
        cost_estimate=pl.CostEstimate(flops=18 * rows * d * ff, bytes_accessed=40 * 2**20, transcendentals=2 * rows * ff),
        name='expert_first' if first else 'expert_next')(*args)


def capacity_of(tok_rows, top_k, experts):
    return 8 * ((5 * tok_rows * top_k + 32 * experts - 1) // (32 * experts))


def positions(own_ref, owners):
    tokens = own_ref.shape[1]
    who = lax.broadcasted_iota(jnp.int32, (owners, tokens), 0)
    chosen = (own_ref[0:1, :] == who) | (own_ref[1:2, :] == who)
    before = lax.broadcasted_iota(jnp.int32, (tokens, tokens), 0) < lax.broadcasted_iota(jnp.int32, (tokens, tokens), 1)
    flags = jnp.where(chosen, 1.0, 0.0).astype(BF16)
    place = jnp.dot(flags, jnp.where(before, 1.0, 0.0).astype(BF16), preferred_element_type=F32)
    return jnp.where(chosen, place, -1.0)


def dispatch_kernel(owners, cap, own_ref, x_ref, dy_ref, xdy_ref, pos_v):
    step = pl.program_id(0)
    d = x_ref.shape[1]

    @pl.when(step == 0)
    def _():
        pos_v[...] = positions(own_ref, owners)

    place = pos_v[pl.ds(step, 1), :].astype(jnp.int32)
    hit = place == lax.broadcasted_iota(jnp.int32, (cap, place.shape[1]), 0)
    pick = jnp.where(hit, 1.0, 0.0).astype(BF16)
    xdy_ref[:, :d] = jnp.dot(pick, x_ref[...], preferred_element_type=F32).astype(BF16)
    xdy_ref[:, d:] = jnp.dot(pick, dy_ref[...], preferred_element_type=F32).astype(BF16)


def dispatch(own_t, x_in, dy_out, mb, owners, cap):
    _, tokens, d = x_in.shape
    part = pl.BlockSpec((None, tokens, d), lambda i: (mb, 0, 0))
    return pl.pallas_call(
        functools.partial(dispatch_kernel, owners, cap),
        grid=(owners,),
        in_specs=[pl.BlockSpec((None, 2, tokens), lambda i: (mb, 0, 0)), part, part],
        out_specs=pl.BlockSpec((cap, 2 * d), lambda i: (i, 0)),
        out_shape=jax.ShapeDtypeStruct((owners * cap, 2 * d), BF16),
        scratch_shapes=[pltpu.VMEM((owners, tokens), F32)],
        compiler_params=pltpu.CompilerParams(vmem_limit_bytes=60 * 2**20),
        cost_estimate=pl.CostEstimate(flops=4 * owners * cap * tokens * d, bytes_accessed=8 * 2**20, transcendentals=0))(own_t, x_in, dy_out)


def gates_kernel(cap, here_sm, table_ref, gate_ref, cols_v, place_v, gate_v):
    blocks, tokens = table_ref.shape[0], table_ref.shape[2]
    here = here_sm[0].astype(F32)
    row = lambda j: jnp.concatenate([table_ref[k, j:j + 1, :] for k in range(blocks)], axis=0)
    first = row(0) == here
    chosen = first | (row(1) == here)
    before = lax.broadcasted_iota(jnp.int32, (tokens, tokens), 0) < lax.broadcasted_iota(jnp.int32, (tokens, tokens), 1)
    flags = jnp.where(chosen, 1.0, 0.0).astype(BF16)
    place = jnp.dot(flags, jnp.where(before, 1.0, 0.0).astype(BF16), preferred_element_type=F32)
    place_v[...] = jnp.where(chosen, place, -1.0).astype(jnp.int32)
    gate_v[...] = jnp.where(first, row(2), row(3))
    cols_v[...] = jnp.zeros_like(cols_v)

    def one(k, c):
        hit = place_v[pl.ds(k, 1), :] == lax.broadcasted_iota(jnp.int32, (cap, tokens), 0)
        column = jnp.sum(jnp.where(hit, gate_v[pl.ds(k, 1), :], 0.0), axis=1, keepdims=True)
        cols_v[...] += jnp.where(lax.broadcasted_iota(jnp.int32, cols_v.shape, 1) == k, column, 0.0)
        return c

    lax.fori_loop(0, blocks, one, 0)
    gate_ref[...] = cols_v[...].T[:blocks, :]


def slot_gates(here, table, cap):
    blocks, _, tokens = table.shape
    vm = pl.BlockSpec(memory_space=pltpu.VMEM)
    return pl.pallas_call(
        functools.partial(gates_kernel, cap),
        in_specs=[pl.BlockSpec(memory_space=pltpu.SMEM), vm],
        out_specs=vm,
        out_shape=jax.ShapeDtypeStruct((blocks, cap), F32),
        scratch_shapes=[pltpu.VMEM((cap, 128), F32), pltpu.VMEM((blocks, tokens), jnp.int32), pltpu.VMEM((blocks, tokens), F32)],
        cost_estimate=pl.CostEstimate(flops=10 * 2**30, bytes_accessed=2**20, transcendentals=0),
        name='slot_gates')(here, table)


def combine_kernel(owners, cap, n_sm, own_ref, dg_ref, *rest):
    backs, (dx_ref, dgate_ref, rows_v, slots_v, pos_v, sem) = rest[:-6], rest[-6:]
    mb = pl.program_id(0)
    for k, back in enumerate(backs):
        @pl.when(mb == k)
        def _(back=back):
            copy = pltpu.make_async_copy(back, rows_v, sem)
            copy.start()
            copy.wait()
    tokens = own_ref.shape[1]
    d = rows_v.shape[1]
    pos_v[...] = positions(own_ref, owners)
    dg_cols = dg_ref[...].T
    place_iota = lax.broadcasted_iota(jnp.int32, (cap, tokens), 0)
    row_iota = lax.broadcasted_iota(jnp.int32, (cap, d), 0)

    def one(k, c):
        dgate, slot = list(c[:2]), list(c[2:])
        place = pos_v[pl.ds(k, 1), :].astype(jnp.int32)
        column = jnp.sum(jnp.where(lax.broadcasted_iota(jnp.int32, dg_cols.shape, 1) == k, dg_cols, 0.0), axis=1, keepdims=True)
        got = jnp.sum(jnp.where(place == place_iota, column, 0.0), axis=0, keepdims=True)
        kept = jnp.where(place < cap, place + k * cap, -1)
        for j in range(2):
            mine = own_ref[j:j + 1, :] == k
            dgate[j] = jnp.where(mine, got, dgate[j])
            slot[j] = jnp.where(mine, kept, slot[j])
        span = pl.ds(pl.multiple_of(k * cap, cap), cap)
        rows_v[span, :] = jnp.where(row_iota < n_sm[mb, k], rows_v[span, :].astype(F32), 0.0).astype(BF16)
        return (*dgate, *slot)

    zero, none = jnp.zeros((1, tokens), F32), jnp.full((1, tokens), -1, jnp.int32)
    out = lax.fori_loop(0, owners, one, (zero, zero, none, none))
    dgate, slot = out[:2], out[2:]
    dgate_ref[0:1, :] = dgate[0]
    dgate_ref[1:2, :] = dgate[1]
    slots_v[...] = jnp.concatenate([s.astype(F32) for s in slot] + [jnp.zeros((6, tokens), F32)], axis=0).T.astype(jnp.int32)
    step = 256

    def part(i, c):
        here = pl.ds(pl.multiple_of(i * step, step), step)
        iota = lax.broadcasted_iota(jnp.int32, (step, owners * cap), 1)
        hit = (slots_v[here, 0:1] == iota) | (slots_v[here, 1:2] == iota)
        pick = jnp.where(hit, 1.0, 0.0).astype(BF16)
        dx_ref[here, :] = jnp.dot(pick, rows_v[...], preferred_element_type=F32).astype(BF16)
        return c

    lax.fori_loop(0, tokens // step, part, 0)


def combine(n_kept, own_t, backs, dg_back, cap):
    rows, d = backs[0].shape
    micro, _, tokens = own_t.shape
    owners = rows // cap
    whole = pl.BlockSpec(memory_space=pl.ANY)
    pair = pl.BlockSpec((None, 2, tokens), lambda i: (i, 0, 0))
    return pl.pallas_call(
        functools.partial(combine_kernel, owners, cap),
        grid=(micro,),
        in_specs=[pl.BlockSpec(memory_space=pltpu.SMEM), pair, pl.BlockSpec((None, owners, cap), lambda i: (i, 0, 0))] + [whole] * micro,
        out_specs=[pl.BlockSpec((None, tokens, d), lambda i: (i, 0, 0)), pair],
        out_shape=[jax.ShapeDtypeStruct((micro, tokens, d), BF16), jax.ShapeDtypeStruct((micro, 2, tokens), F32)],
        scratch_shapes=[pltpu.VMEM((rows, d), BF16), pltpu.VMEM((tokens, 8), jnp.int32), pltpu.VMEM((owners, tokens), F32), pltpu.SemaphoreType.DMA],
        compiler_params=pltpu.CompilerParams(vmem_limit_bytes=60 * 2**20),
        cost_estimate=pl.CostEstimate(flops=2 * micro * rows * tokens * d, bytes_accessed=12 * 2**20, transcendentals=0),
        name='combine')(n_kept, own_t, dg_back, *backs)


def solution(mesh):
    side = round(mesh.shape['fsdp'] ** (1 / 3))
    cores = mesh.shape['ep']
    grid_mesh = Mesh(mesh.devices.reshape(side, side, side, cores), ('z', 'y', 'x', 'c'))
    tok_spec = P(None, ('z', 'y', 'x', 'c'), None)
    spec_edf = P('c', ('z', 'y', 'x'), None)
    spec_efd = P('c', None, ('z', 'y', 'x'))
    ring = ('x', 'c')

    def local_step(x_in, dy_out, expert_idx, gate_prob, w_one, w_two, w_three):
        micro_count, tok_rows, d_model = x_in.shape
        top_k = expert_idx.shape[2]
        local_experts, shard, ff = w_one.shape
        experts = local_experts * cores
        cap = capacity_of(tok_rows, top_k, experts)
        rows = experts * cap
        ids_t = jnp.transpose(expert_idx, (0, 2, 1))
        own_t = (ids_t % local_experts) * cores + ids_t // local_experts
        q_t = jnp.transpose(gate_prob, (0, 2, 1))
        here = lax.axis_index('x') * cores + lax.axis_index('c')
        mine = jnp.concatenate([own_t.astype(F32), q_t], axis=1)
        tables = [mine]
        for k in range(1, experts):
            tables.append(lax.ppermute(mine, ring, [(i, (i + k) % experts) for i in range(experts)]))
        table = jnp.stack(tables, axis=1).reshape(micro_count * experts, 2 * top_k, tok_rows)
        source = jnp.arange(experts, dtype=jnp.int32)
        is_from = (here - source[:, None]) % experts == source[None, :]
        n_here = jnp.sum((table[:, :top_k] == here.astype(F32)).astype(jnp.int32), axis=(1, 2)).reshape(micro_count, 1, experts)
        n_here = jnp.sum(jnp.where(is_from, n_here, 0), axis=2)
        n_recv = (jnp.minimum(n_here, cap) + UNIT - 1) // UNIT
        picks = (own_t[:, :, :, None] == jnp.arange(experts, dtype=jnp.int32)).astype(jnp.int32)
        n_kept = jnp.minimum(jnp.sum(picks, axis=(1, 2)), cap)
        w_cat = jnp.concatenate([w_one, jnp.transpose(w_two, (0, 2, 1)), w_three], axis=2)
        x_id = lax.axis_index('x')

        def deal(slabs):
            dealt = [lax.dynamic_index_in_dim(slabs, x_id, 0, keepdims=False)]
            for k in range(1, local_experts):
                piece = lax.dynamic_index_in_dim(slabs, (x_id + k) % local_experts, 0, keepdims=False)
                dealt.append(lax.ppermute(piece, 'x', [(i, (i + k) % local_experts) for i in range(local_experts)]))
            result = []
            for j in range(local_experts):
                back = (x_id - j) % local_experts
                slab = dealt[0]
                for k in range(1, local_experts):
                    slab = jnp.where(back == k, dealt[k], slab)
                result.append(slab)
            return result

        w_mine = jnp.concatenate(deal(w_cat), axis=0)
        w_full = lax.all_gather(w_mine, ('z', 'y'), axis=0, tiled=True)
        xdy = []
        for mb in range(micro_count):
            send = dispatch(own_t, x_in, dy_out, mb, experts, cap)
            xdy.append(lax.all_to_all(send.reshape(experts, cap, 2 * d_model), ring, 0, 0, tiled=True).reshape(rows, 2 * d_model))
        gate_rows = slot_gates(here.reshape(1), table, cap).reshape(micro_count, 1, experts, cap)
        gate_rows = jnp.sum(jnp.where(is_from[:, :, None], gate_rows, 0.0), axis=2)
        dx_back = []
        dg_rows = []
        grad_sum = None
        for mb in range(micro_count):
            dx_rows, dg, grad_sum = expert_pass(n_recv[mb], xdy[mb], gate_rows[mb], w_full, grad_sum)
            dx_back.append(lax.all_to_all(dx_rows.reshape(experts, cap, d_model), ring, 0, 0, tiled=True).reshape(rows, d_model))
            dg_rows.append(dg)
        dw_mine = lax.psum_scatter(grad_sum, ('z', 'y'), scatter_dimension=0, tiled=True)
        dg_back = lax.all_to_all(jnp.stack(dg_rows, axis=1), ring, 0, 0, tiled=True)
        done = combine(n_kept, own_t, dx_back, jnp.transpose(dg_back, (1, 0, 2)), cap)
        dx_in, d_gate = done[0], jnp.transpose(done[1], (0, 2, 1))
        dw_all = jnp.stack(deal(dw_mine.reshape(local_experts, shard, 3 * ff)))
        dw_one, dw_two, dw_three = dw_all[:, :, :ff], jnp.transpose(dw_all[:, :, ff:2 * ff], (0, 2, 1)), dw_all[:, :, 2 * ff:]
        return dx_in, d_gate, dw_one, dw_two, dw_three

    return jax.shard_map(local_step, mesh=grid_mesh, in_specs=(tok_spec, tok_spec, tok_spec, tok_spec, spec_edf, spec_efd, spec_edf), out_specs=(tok_spec, tok_spec, spec_edf, spec_efd, spec_edf), check_vma=False)
```

profile of v0, /device:TPU:0, one launch (start us, length us, event | category | flops | bytes accessed | tf_op | source)
XLA Modules:
  0.0 360.4 jit_solution(14722076876750183462)
XLA Ops:
  7.3 1.0 pad_maximum_fusion.1
  8.3 2.9 collective-permute-start.7
  12.1 0.9 collective-permute-start.9
  13.0 2.0 collective-permute-done.7
  14.9 2.8 collective-permute-done.8
  17.7 0.9 collective-permute-done.9
  19.4 1.4 fusion.23
  20.8 9.6 %shard_map.110 = bf16[2560,1024]{1,0:T(8,128)(2,1)} custom-call(s32[2,2,1024]{2,1,0:T(2,128)} %get-tuple-element.22.own_ref, bf16[2,1024,512]{2,1,0:T(8,128)(2,1)} %x_ref.3, bf16[2,1024,512]{2,1,0:T(8,128)(2,1)} %dy_ref.3), custom_call_target="tpu_custom_call" | custom-call | flops 5368709120 | bytes 8388608 | tf_op jit(solution)/shard_map/pallas_call | solution.py:207
  30.4 4.8 %all-to-all-start = ((bf16[8,320,1024]{2,1,0:T(8,128)(2,1)}), bf16[8,320,1024]{2,1,0:T(8,128)(2,1)}, u32[]{:S(2)}, u32[]{:S(2)}) async-start(bf16[8,320,1024]{2,1,0:T(8,128)(2,1)} %bitcast.127), calls=%async_computation | async-start | bytes 10485760 | tf_op jit(solution)/shard_map/all_to_all | solution.py:375
  35.6 1.6 collective-permute-start.1
  37.3 2.0 collective-permute-start.2
  39.2 2.0 collective-permute-start.3
  41.3 1.7 collective-permute-start.4
  43.0 9.6 %shard_map.111 = bf16[2560,1024]{1,0:T(8,128)(2,1)} custom-call(s32[2,2,1024]{2,1,0:T(2,128)} %get-tuple-element.22.own_ref, bf16[2,1024,512]{2,1,0:T(8,128)(2,1)} %x_ref.3, bf16[2,1024,512]{2,1,0:T(8,128)(2,1)} %dy_ref.3), custom_call_target="tpu_custom_call" | custom-call | flops 5368709120 | bytes 8388608 | tf_op jit(solution)/shard_map/pallas_call | solution.py:207
  52.7 28.8 %collective-permute-done = f32[2,4,1024]{2,1,0:T(4,128)S(1)} collective-permute-done((f32[2,4,1024]{2,1,0:T(4,128)S(1)}, f32[2,4,1024]{2,1,0:T(4,128)S(1)}, u32[]{:S(2)}, u32[]{:S(2)}) %collective-permute-start) | collective-permute-done | bytes 32800 | tf_op jit(solution)/shard_map/ppermute | solution.py:344
  81.4 15.3 %collective-permute-start.5 = (f32[2,4,1024]{2,1,0:T(4,128)S(1)}, f32[2,4,1024]{2,1,0:T(4,128)S(1)}, u32[]{:S(2)}, u32[]{:S(2)}) collective-permute-start(f32[2,4,1024]{2,1,0:T(4,128)S(1)} %pad_maximum_fusion.3), channel_id=1, source_target_pairs={{0,6},{1,7},{2,0},{3,1},{4,2},{5,3},{6,4},{7,5},{8,14},{9,15},{10,... | collective-permute-start | bytes 98312 | tf_op jit(solution)/shard_map/ppermute | solution.py:344
  97.6 0.9 collective-permute-done.3
  99.0 0.9 copy.19.table_ref
  100.2 6.1 %slot_gates.1 = f32[16,320]{1,0:T(8,128)} custom-call(s32[1]{0:T(128)} %bitcast.14.here_sm, f32[16,4,1024]{2,1,0:T(4,128)} %copy.19.table_ref), custom_call_target="tpu_custom_call" | custom-call | flops 10737418240 | bytes 1048576 | tf_op jit(solution)/shard_map/slot_gates/pallas_call | solution.py:244
  107.2 4.7 %all-to-all-start.1 = ((bf16[8,320,1024]{2,1,0:T(8,128)(2,1)}), bf16[8,320,1024]{2,1,0:T(8,128)(2,1)}, u32[]{:S(2)}, u32[]{:S(2)}) async-start(bf16[8,320,1024]{2,1,0:T(8,128)(2,1)} %bitcast.128), calls=%async_computation.1 | async-start | bytes 10485760 | tf_op jit(solution)/shard_map/all_to_all | solution.py:375
  113.1 39.0 %expert_first.1 = (bf16[2560,512]{1,0:T(8,128)(2,1)}, f32[8,320]{1,0:T(8,128)}, f32[512,5376]{1,0:T(8,128)}) custom-call(s32[8]{0:T(128)} %get-tuple-element.42.n_sm, bf16[2560,1024]{1,0:T(8,128)(2,1)} %bitcast.13.xdy_hbm, f32[8,320]{1,0:T(8,128)} %get-tuple-element.40.q_ref, bf16[512,5376]{1,0:T(8,128)(2,1)} %all-gather.2.cloned.1.call-done.w_hbm), custom_call_target="tpu_custom_call" | custom-call | flops 42278584320 | bytes 41943040 | tf_op jit(solution)/shard_map/expert_first/pallas_call | solution.py:165
  152.2 20.6 %all-to-all-done.1 = bf16[8,320,1024]{2,1,0:T(8,128)(2,1)} async-done(((bf16[8,320,1024]{2,1,0:T(8,128)(2,1)}), bf16[8,320,1024]{2,1,0:T(8,128)(2,1)}, u32[]{:S(2)}, u32[]{:S(2)}) %all-to-all-start.1) | async-done | bytes 5242912 | tf_op jit(solution)/shard_map/all_to_all | solution.py:375
  172.8 39.7 %expert_next.1 = (bf16[2560,512]{1,0:T(8,128)(2,1)}, f32[8,320]{1,0:T(8,128)}, f32[512,5376]{1,0:T(8,128)}) custom-call(s32[8]{0:T(128)} %get-tuple-element.43.n_sm, bf16[2560,1024]{1,0:T(8,128)(2,1)} %bitcast.25.xdy_hbm, f32[8,320]{1,0:T(8,128)} %get-tuple-element.41.q_ref, bf16[512,5376]{1,0:T(8,128)(2,1)} %all-gather.2.cloned.1.call-done.w_hbm, ...), custom_call_target="tpu_custom_call" | custom-call | flops 42278584320 | bytes 41943040 | tf_op jit(solution)/shard_map/expert_next/pallas_call | solution.py:165
  213.2 27.8 %all_to_all.25 = f32[8,2,320]{2,1,0:T(2,128)S(1)} all-to-all(f32[8,2,320]{2,1,0:T(2,128)S(1)} %copy.20), channel_id=1, replica_groups=mesh['z'=4,'y'=4,'x'=4,'c'=2] {'x','c'}, dimensions={0} | all-to-all | bytes 40960 | tf_op jit(solution)/shard_map/all_to_all | solution.py:386
  240.9 36.1 %all_to_all.26 = bf16[8,320,512]{2,1,0:T(8,128)(2,1)} all-to-all(bf16[8,320,512]{2,1,0:T(8,128)(2,1)S(1)} %bitcast.131), channel_id=1, replica_groups=mesh['z'=4,'y'=4,'x'=4,'c'=2] {'x','c'}, dimensions={0} | all-to-all | bytes 5242880 | tf_op jit(solution)/shard_map/all_to_all | solution.py:383
  277.1 3.6 %all-to-all-start.3 = ((bf16[8,320,512]{2,1,0:T(8,128)(2,1)}), bf16[8,320,512]{2,1,0:T(8,128)(2,1)S(1)}, u32[]{:S(2)}, u32[]{:S(2)}) async-start(bf16[8,320,512]{2,1,0:T(8,128)(2,1)} %bitcast.29), calls=%async_computation.3 | async-start | bytes 5242880 | tf_op jit(solution)/shard_map/all_to_all | solution.py:383
  282.1 41.5 %reduce-scatter.2.cloned.1.call-done = f32[32,5376]{1,0:T(8,128)} async-done(((f32[512,5376]{1,0:T(8,128)}), f32[32,5376]{1,0:T(8,128)}) %reduce-scatter.2.cloned.1.call-update) | async-done | bytes 688144 | tf_op jit(solution)/shard_map/reduce_scatter | solution.py:385
  323.6 1.8 dynamic-slice_bitcast_fusion
  325.4 2.7 collective-permute-start.10
  329.8 1.5 copy-done
  331.3 20.3 %combine.1 = (bf16[2,1024,512]{2,1,0:T(8,128)(2,1)}, f32[2,2,1024]{2,1,0:T(2,128)}) custom-call(s32[2,8]{1,0:T(2,128)} %broadcast_minimum_fusion.n_sm, s32[2,2,1024]{2,1,0:T(2,128)} %get-tuple-element.22.own_ref, f32[2,8,320]{2,1,0:T(8,128)} %bitcast.139, bf16[2560,512]{1,0:T(8,128)(2,1)} %bitcast.130, bf16[2560,512]{1,0:T(8,128)(2,1)} %bitcast.129), custom_call_target="tpu_custom_call" | custom-call | flops 5368709120 | bytes 12582912 | tf_op jit(solution)/shard_map/combine/pallas_call | solution.py:309
  351.7 1.0 fusion.2
  (60 shorter events, 10.7 us)
Async XLA Ops:
  7.2 106.0 %all-gather.2.cloned.1.call-start = ((), (), s32[]{:S(2)}) async-start(), calls=%async_computation.6 | async-start | bytes 5849088 | tf_op jit(solution)/shard_map/all_gather | solution.py:371
  8.3 6.6 %collective-permute-start.7 = (bf16[8,5376]{1,0:T(8,128)(2,1)S(1)}, bf16[8,5376]{1,0:T(8,128)(2,1)S(1)}, u32[]{:S(2)}, u32[]{:S(2)}) collective-permute-start(bf16[8,5376]{1,0:T(8,128)(2,1)S(1)} %get-tuple-element.39), channel_id=1, source_target_pairs={{0,6},{2,0},{4,2},{6,4},{1,7},{3,1},{5,3},{7,5},{8,14},{10,8},{12,... | collective-permute-start | bytes 258056 | tf_op jit(solution)/shard_map/ppermute | solution.py:360
  11.3 6.4 %collective-permute-start.8 = (bf16[8,5376]{1,0:T(8,128)(2,1)S(1)}, bf16[8,5376]{1,0:T(8,128)(2,1)S(1)}, u32[]{:S(2)}, u32[]{:S(2)}) collective-permute-start(bf16[8,5376]{1,0:T(8,128)(2,1)S(1)} %get-tuple-element.38), channel_id=1, source_target_pairs={{0,4},{2,6},{4,0},{6,2},{1,5},{3,7},{5,1},{7,3},{8,12},{10,14},{12... | collective-permute-start | bytes 258056 | tf_op jit(solution)/shard_map/ppermute | solution.py:360
  12.1 6.5 %collective-permute-start.9 = (bf16[8,5376]{1,0:T(8,128)(2,1)S(1)}, bf16[8,5376]{1,0:T(8,128)(2,1)S(1)}, u32[]{:S(2)}, u32[]{:S(2)}) collective-permute-start(bf16[8,5376]{1,0:T(8,128)(2,1)S(1)} %get-tuple-element.37), channel_id=1, source_target_pairs={{0,2},{2,4},{4,6},{6,0},{1,3},{3,5},{5,7},{7,1},{8,10},{10,12},{12... | collective-permute-start | bytes 258056 | tf_op jit(solution)/shard_map/ppermute | solution.py:360
  30.4 4.8 %copy-start.3 = (f32[2,1024,2]{1,2,0:T(2,128)S(1)}, f32[2,1024,2]{1,2,0:T(2,128)}, u32[]{:S(2)}) copy-start(f32[2,1024,2]{1,2,0:T(2,128)} %param.10) | copy-start | bytes 49156
  30.4 76.8 %all-to-all-start = ((bf16[8,320,1024]{2,1,0:T(8,128)(2,1)}), bf16[8,320,1024]{2,1,0:T(8,128)(2,1)}, u32[]{:S(2)}, u32[]{:S(2)}) async-start(bf16[8,320,1024]{2,1,0:T(8,128)(2,1)} %bitcast.127), calls=%async_computation | async-start | bytes 10485760 | tf_op jit(solution)/shard_map/all_to_all | solution.py:375
  35.2 46.2 %collective-permute-start = (f32[2,4,1024]{2,1,0:T(4,128)S(1)}, f32[2,4,1024]{2,1,0:T(4,128)S(1)}, u32[]{:S(2)}, u32[]{:S(2)}) collective-permute-start(f32[2,4,1024]{2,1,0:T(4,128)S(1)} %pad_maximum_fusion.3), channel_id=1, source_target_pairs={{0,1},{1,2},{2,3},{3,4},{4,5},{5,6},{6,7},{7,0},{8,9},{9,10},{10,1... | collective-permute-start | bytes 98312 | tf_op jit(solution)/shard_map/ppermute | solution.py:344
  35.6 61.1 %collective-permute-start.1 = (f32[2,4,1024]{2,1,0:T(4,128)S(1)}, f32[2,4,1024]{2,1,0:T(4,128)S(1)}, u32[]{:S(2)}, u32[]{:S(2)}) collective-permute-start(f32[2,4,1024]{2,1,0:T(4,128)S(1)} %pad_maximum_fusion.3), channel_id=1, source_target_pairs={{0,2},{1,3},{2,4},{3,5},{4,6},{5,7},{6,0},{7,1},{8,10},{9,11},{10,... | collective-permute-start | bytes 98312 | tf_op jit(solution)/shard_map/ppermute | solution.py:344
  37.3 60.3 %collective-permute-start.2 = (f32[2,4,1024]{2,1,0:T(4,128)S(1)}, f32[2,4,1024]{2,1,0:T(4,128)S(1)}, u32[]{:S(2)}, u32[]{:S(2)}) collective-permute-start(f32[2,4,1024]{2,1,0:T(4,128)S(1)} %pad_maximum_fusion.3), channel_id=1, source_target_pairs={{0,3},{1,4},{2,5},{3,6},{4,7},{5,0},{6,1},{7,2},{8,11},{9,12},{10,... | collective-permute-start | bytes 98312 | tf_op jit(solution)/shard_map/ppermute | solution.py:344
  39.2 59.2 %collective-permute-start.3 = (f32[2,4,1024]{2,1,0:T(4,128)S(1)}, f32[2,4,1024]{2,1,0:T(4,128)S(1)}, u32[]{:S(2)}, u32[]{:S(2)}) collective-permute-start(f32[2,4,1024]{2,1,0:T(4,128)S(1)} %pad_maximum_fusion.3), channel_id=1, source_target_pairs={{0,4},{1,5},{2,6},{3,7},{4,0},{5,1},{6,2},{7,3},{8,12},{9,13},{10,... | collective-permute-start | bytes 98312 | tf_op jit(solution)/shard_map/ppermute | solution.py:344
  41.3 57.2 %collective-permute-start.4 = (f32[2,4,1024]{2,1,0:T(4,128)S(1)}, f32[2,4,1024]{2,1,0:T(4,128)S(1)}, u32[]{:S(2)}, u32[]{:S(2)}) collective-permute-start(f32[2,4,1024]{2,1,0:T(4,128)S(1)} %pad_maximum_fusion.3), channel_id=1, source_target_pairs={{0,5},{1,6},{2,7},{3,0},{4,1},{5,2},{6,3},{7,4},{8,13},{9,14},{10,... | collective-permute-start | bytes 98312 | tf_op jit(solution)/shard_map/ppermute | solution.py:344
  81.4 17.1 %collective-permute-start.5 = (f32[2,4,1024]{2,1,0:T(4,128)S(1)}, f32[2,4,1024]{2,1,0:T(4,128)S(1)}, u32[]{:S(2)}, u32[]{:S(2)}) collective-permute-start(f32[2,4,1024]{2,1,0:T(4,128)S(1)} %pad_maximum_fusion.3), channel_id=1, source_target_pairs={{0,6},{1,7},{2,0},{3,1},{4,2},{5,3},{6,4},{7,5},{8,14},{9,15},{10,... | collective-permute-start | bytes 98312 | tf_op jit(solution)/shard_map/ppermute | solution.py:344
  96.8 2.1 collective-permute-start.6
  107.2 65.5 %all-to-all-start.1 = ((bf16[8,320,1024]{2,1,0:T(8,128)(2,1)}), bf16[8,320,1024]{2,1,0:T(8,128)(2,1)}, u32[]{:S(2)}, u32[]{:S(2)}) async-start(bf16[8,320,1024]{2,1,0:T(8,128)(2,1)} %bitcast.128), calls=%async_computation.1 | async-start | bytes 10485760 | tf_op jit(solution)/shard_map/all_to_all | solution.py:375
  111.9 211.7 %reduce-scatter.2.cloned.1.call-start = ((), (), s32[]{:S(2)}) async-start(), calls=%async_computation.7 | async-start | bytes 11698176 | tf_op jit(solution)/shard_map/reduce_scatter | solution.py:385
  212.4 0.7 copy-start.4
  212.5 0.7 copy-start.5
  212.5 28.5 %copy-start.1 = (bf16[2560,512]{1,0:T(8,128)(2,1)S(1)}, bf16[2560,512]{1,0:T(8,128)(2,1)}, u32[]{:S(2)}) copy-start(bf16[2560,512]{1,0:T(8,128)(2,1)} %get-tuple-element.17) | copy-start | bytes 7864324
  240.9 39.8 %copy-start.2 = (s32[2,2,1024]{2,1,0:T(2,128)S(1)}, s32[2,2,1024]{2,1,0:T(2,128)}, u32[]{:S(2)}) copy-start(s32[2,2,1024]{2,1,0:T(2,128)} %get-tuple-element.22.own_ref) | copy-start | bytes 49156
  277.1 52.7 %all-to-all-start.3 = ((bf16[8,320,512]{2,1,0:T(8,128)(2,1)}), bf16[8,320,512]{2,1,0:T(8,128)(2,1)S(1)}, u32[]{:S(2)}, u32[]{:S(2)}) async-start(bf16[8,320,512]{2,1,0:T(8,128)(2,1)} %bitcast.29), calls=%async_computation.3 | async-start | bytes 5242880 | tf_op jit(solution)/shard_map/all_to_all | solution.py:383
  325.4 26.3 %collective-permute-start.10 = (f32[8,5376]{1,0:T(8,128)}, f32[8,5376]{1,0:T(8,128)S(1)}, u32[]{:S(2)}, u32[]{:S(2)}) collective-permute-start(f32[8,5376]{1,0:T(8,128)} %get-tuple-element.32), channel_id=1, source_target_pairs={{0,6},{2,0},{4,2},{6,4},{1,7},{3,1},{5,3},{7,5},{8,14},{10,8},{12,... | collective-permute-start | bytes 516104 | tf_op jit(solution)/shard_map/ppermute | solution.py:360
  328.1 23.5 %collective-permute-start.11 = (f32[8,5376]{1,0:T(8,128)S(1)}, f32[8,5376]{1,0:T(8,128)S(1)}, u32[]{:S(2)}, u32[]{:S(2)}) collective-permute-start(f32[8,5376]{1,0:T(8,128)S(1)} %get-tuple-element.31), channel_id=1, source_target_pairs={{0,4},{2,6},{4,0},{6,2},{1,5},{3,7},{5,1},{7,3},{8,12},{10,14},{12... | collective-permute-start | bytes 516104 | tf_op jit(solution)/shard_map/ppermute | solution.py:360
  328.9 22.7 %collective-permute-start.12 = (f32[8,5376]{1,0:T(8,128)S(1)}, f32[8,5376]{1,0:T(8,128)S(1)}, u32[]{:S(2)}, u32[]{:S(2)}) collective-permute-start(f32[8,5376]{1,0:T(8,128)S(1)} %get-tuple-element.30), channel_id=1, source_target_pairs={{0,2},{2,4},{4,6},{6,0},{1,3},{3,5},{5,7},{7,1},{8,10},{10,12},{12... | collective-permute-start | bytes 516104 | tf_op jit(solution)/shard_map/ppermute | solution.py:360
  329.8 1.5 copy-start
Sparse Core Ops, SparseCore 0:
  19.6 57.7 all-gather.1
  212.6 110.9 reduce-scatter.1
where the time goes:
time: 362 us; the launch traced here: 360 us
  Pallas kernels  124 us (34%)
  waiting for transfers between devices  98.1 us (27%)
  blocking collectives  63.9 us (18%)
  starting transfers between devices  45.7 us (13%)
  between operations  14.3 us (4%)
  local copies, waits for them, and re-layouts  7.86 us (2%)
  other arithmetic  6.27 us (2%)
    pallas_call x2, Pallas kernels, expert_pass(): pl.pallas_call(functools.partial(expert_kernel, ff, cap, first), in_specs...  78.7 us
    reduce_scatter x1, waiting for transfers between devices, local_step(): lax.psum_scatter(grad_sum, ('z', 'y'), scatter_dimension=0, tiled=True)  41.5 us
    all_to_all x1, blocking collectives, local_step(): lax.all_to_all(dx_rows.reshape(experts, cap, d_model), ring, 0, 0, tiled=...  36.1 us
    ppermute x7, waiting for transfers between devices, local_step(): lax.ppermute(mine, ring, [(i, (i + k) % experts) for i in range(experts)])  30.3 us
    all_to_all x1, blocking collectives, local_step(): dg_back = lax.all_to_all(jnp.stack(dg_rows, axis=1), ring, 0, 0, tiled=True)  27.8 us
    ppermute x7, starting transfers between devices, local_step(): lax.ppermute(mine, ring, [(i, (i + k) % experts) for i in range(experts)])  23.5 us
    all_to_all x2, waiting for transfers between devices, local_step(): lax.all_to_all(send.reshape(experts, cap, 2 * d_model), ring, 0, 0, tiled...  20.6 us
    pallas_call x1, Pallas kernels, combine(): pl.pallas_call(functools.partial(combine_kernel, owners, cap), grid=(micr...  20.3 us
  transfers between devices with their start and end apart: 18, of which 9 were waited for; matrix products, arithmetic and copies ran while one was open for 2% of the time, Pallas kernels for 23%

commit v1 on v0

--- a/solution.py
+++ b/solution.py
@@ -22,24 +22,25 @@
         for k in range(cap // 64):
             @pl.when((k + 1) * 4 <= n)
             def _(k=k, s=s, off=off):
-                emit(s * cap + k * 64, off * UNIT + k * 64, 64)
+                emit(s, k * 64, off * UNIT + k * 64, 64)
         base = (n // 4) * 4
 
         @pl.when((n // 2) % 2 == 1)
         def _(s=s, off=off, base=base):
-            emit(s * cap + base * UNIT, (off + base) * UNIT, 32)
+            emit(s, base * UNIT, (off + base) * UNIT, 32)
 
         tail = (n // 2) * 2
 
         @pl.when(n % 2 == 1)
         def _(s=s, off=off, tail=tail):
-            emit(s * cap + tail * UNIT, (off + tail) * UNIT, 16)
+            emit(s, tail * UNIT, (off + tail) * UNIT, 16)
 
         off = off + n
     return off
 
 
-def expert_kernel(ff, cap, first, n_sm, xdy_hbm, q_ref, w_hbm, *rest):
+def expert_kernel(ff, cap, first, blocks, n_sm, src_sm, *rest):
+    xdy_hbm, (q_ref, w_hbm), rest = rest[:blocks], rest[blocks:blocks + 2], rest[blocks + 2:]
     if first:
         dx_hbm, dg_ref, gw_hbm, xdy_v, q_v, dg_v, dx_v, w_v, gw_v, xt_v, gt_v, sems = rest
         gin_hbm = gin_v = None
@@ -51,8 +52,9 @@
     def m8(v, n=UNIT):
         return v if isinstance(v, int) else pl.multiple_of(v, n)
 
-    def fetch(slot, packed, size):
-        return pltpu.make_async_copy(xdy_hbm.at[pl.ds(m8(slot), size)], xdy_v.at[pl.ds(m8(packed), size)], sems.at[0])
+    def fetch(s, row, packed, size):
+        source, row = (xdy_hbm[0], s * cap + row) if blocks == 1 else (xdy_hbm[s], row)
+        return pltpu.make_async_copy(source.at[pl.ds(m8(row), size)], xdy_v.at[pl.ds(m8(packed), size)], sems.at[0])
 
     units = row_pieces(n_sm, cap, lambda *a: fetch(*a).start())
     parts = [pltpu.make_async_copy(w_hbm.at[:, pl.ds(k * ff, ff)], w_v.at[:, pl.ds(k * ff, ff)], sems.at[1 + k]) for k in range(3)]
@@ -130,8 +132,8 @@
         o.start()
         outs.append(o)
 
-    def put(slot, packed, size):
-        return pltpu.make_async_copy(dx_v.at[pl.ds(m8(packed), size)], dx_hbm.at[pl.ds(m8(slot), size)], sems.at[0])
+    def put(s, row, packed, size):
+        return pltpu.make_async_copy(dx_v.at[pl.ds(m8(packed), size)], dx_hbm.at[pl.ds(m8(src_sm[s] * cap + row), size)], sems.at[0])
 
     row_pieces(n_sm, cap, lambda *a: put(*a).start())
     off = jnp.int32(0)
@@ -145,16 +147,18 @@
         o.wait()
 
 
-def expert_pass(n_units, xdy, gates, w_full, grad_in):
-    rows, d2 = xdy.shape
+def expert_pass(n_units, sources, xdy, gates, w_full, grad_in):
+    d2 = xdy[0].shape[1]
+    rows = sum(block.shape[0] for block in xdy)
     d = d2 // 2
     ff = w_full.shape[1] // 3
     cap = gates.shape[1]
     first = grad_in is None
     whole = pl.BlockSpec(memory_space=pl.ANY)
     vm = pl.BlockSpec(memory_space=pltpu.VMEM)
-    args = [n_units, xdy, gates, w_full] + ([] if first else [grad_in])
-    in_specs = [pl.BlockSpec(memory_space=pltpu.SMEM), whole, vm, whole] + ([] if first else [whole])
+    args = [n_units, sources, *xdy, gates, w_full] + ([] if first else [grad_in])
+    smem = pl.BlockSpec(memory_space=pltpu.SMEM)
+    in_specs = [smem, smem] + [whole] * len(xdy) + [vm, whole] + ([] if first else [whole])
     pad = rows + 512
     scratch = [
         pltpu.VMEM((rows, d2), BF16), pltpu.VMEM((pad, 1), F32), pltpu.VMEM((pad, 1), F32), pltpu.VMEM((rows, d), BF16),
@@ -163,7 +167,7 @@
         scratch.append(pltpu.VMEM((d, 3 * ff), F32))
     scratch.append(pltpu.SemaphoreType.DMA((5,)))
     return pl.pallas_call(
-        functools.partial(expert_kernel, ff, cap, first),
+        functools.partial(expert_kernel, ff, cap, first, len(xdy)),
         in_specs=in_specs, out_specs=[whole, vm, whole],
         out_shape=[jax.ShapeDtypeStruct((rows, d), BF16), jax.ShapeDtypeStruct(gates.shape, F32), jax.ShapeDtypeStruct((d, 3 * ff), F32)],
         scratch_shapes=scratch,
@@ -346,8 +350,9 @@
         source = jnp.arange(experts, dtype=jnp.int32)
         is_from = (here - source[:, None]) % experts == source[None, :]
         n_here = jnp.sum((table[:, :top_k] == here.astype(F32)).astype(jnp.int32), axis=(1, 2)).reshape(micro_count, 1, experts)
-        n_here = jnp.sum(jnp.where(is_from, n_here, 0), axis=2)
-        n_recv = (jnp.minimum(n_here, cap) + UNIT - 1) // UNIT
+        n_near = (jnp.minimum(n_here, cap) + UNIT - 1) // UNIT
+        n_recv = [jnp.sum(jnp.where(is_from, n_near[0], 0), axis=1), n_near[1, 0]]
+        came = [source, (here - source) % experts]
         picks = (own_t[:, :, :, None] == jnp.arange(experts, dtype=jnp.int32)).astype(jnp.int32)
         n_kept = jnp.minimum(jnp.sum(picks, axis=(1, 2)), cap)
         w_cat = jnp.concatenate([w_one, jnp.transpose(w_two, (0, 2, 1)), w_three], axis=2)
@@ -372,16 +377,24 @@
         xdy = []
         for mb in range(micro_count):
             send = dispatch(own_t, x_in, dy_out, mb, experts, cap)
-            xdy.append(lax.all_to_all(send.reshape(experts, cap, 2 * d_model), ring, 0, 0, tiled=True).reshape(rows, 2 * d_model))
-        gate_rows = slot_gates(here.reshape(1), table, cap).reshape(micro_count, 1, experts, cap)
-        gate_rows = jnp.sum(jnp.where(is_from[:, :, None], gate_rows, 0.0), axis=2)
+            send = send.reshape(experts, cap, 2 * d_model)
+            if mb == 0:
+                xdy.append([lax.all_to_all(send, ring, 0, 0, tiled=True).reshape(rows, 2 * d_model)])
+                continue
+            blocks = []
+            for k in range(experts):
+                block = lax.dynamic_index_in_dim(send, (here + k) % experts, 0, keepdims=False)
+                blocks.append(lax.ppermute(block, ring, [(i, (i + k) % experts) for i in range(experts)]) if k else block)
+            xdy.append(blocks)
+        gate_rows = slot_gates(here.reshape(1), table, cap).reshape(micro_count, experts, cap)
+        gate_rows = [jnp.sum(jnp.where(is_from[:, :, None], gate_rows[0], 0.0), axis=1), gate_rows[1]]
         dx_back = []
         dg_rows = []
         grad_sum = None
         for mb in range(micro_count):
-            dx_rows, dg, grad_sum = expert_pass(n_recv[mb], xdy[mb], gate_rows[mb], w_full, grad_sum)
+            dx_rows, dg, grad_sum = expert_pass(n_recv[mb], came[mb], xdy[mb], gate_rows[mb], w_full, grad_sum)
             dx_back.append(lax.all_to_all(dx_rows.reshape(experts, cap, d_model), ring, 0, 0, tiled=True).reshape(rows, d_model))
-            dg_rows.append(dg)
+            dg_rows.append(dg if mb == 0 else jnp.sum(jnp.where(is_from[:, :, None], dg[None], 0.0), axis=1))
         dw_mine = lax.psum_scatter(grad_sum, ('z', 'y'), scatter_dimension=0, tiled=True)
         dg_back = lax.all_to_all(jnp.stack(dg_rows, axis=1), ring, 0, 0, tiled=True)
         done = combine(n_kept, own_t, dx_back, jnp.transpose(dg_back, (1, 0, 2)), cap)

time: 362 us -> 369 us (1.019)
  waiting for transfers between devices: 98.1 us -> 84.2 us
  local copies, waits for them, and re-layouts: 7.86 us -> 17.8 us
  blocking collectives: 63.9 us -> 73.1 us
    all_to_all x2 -> x1, waiting for transfers between devices: 20.6 us -> 0.01 us  [local_step(): lax.all_to_all(send, ring, 0, 0, tiled=True).reshape(rows, 2 * d_model)]
    ppermute x0 -> x7, starting transfers between devices: none -> 19.2 us  [local_step(): lax.ppermute(block, ring, [(i, (i + k) % experts) for i in range(experts)])]
    ppermute x7, starting transfers between devices: 23.5 us -> 8.32 us  [local_step(): lax.ppermute(mine, ring, [(i, (i + k) % experts) for i in range(experts)])]
    all_to_all x1, blocking collectives: 27.8 us -> 37 us  [local_step(): dg_back = lax.all_to_all(jnp.stack(dg_rows, axis=1), ring, 0, 0, tiled=True)]
    ppermute x7, waiting for transfers between devices: 30.3 us -> 36.2 us  [local_step(): lax.ppermute(mine, ring, [(i, (i + k) % experts) for i in range(experts)])]
    all_to_all x2 -> x1, starting transfers between devices: 9.42 us -> 4.64 us  [local_step(): lax.all_to_all(send, ring, 0, 0, tiled=True).reshape(rows, 2 * d_model)]
    unnamed x18 -> x24, local copies, waits for them, and re-layouts: 2.26 us -> 6.55 us
  transfers between devices with their start and end apart: 18 -> 24, of which waited for: 9 -> 5; matrix products, arithmetic and copies ran while one was open for 2% -> 5% of each run, Pallas kernels for 23% -> 23%
where the time goes in v1:
time: 369 us; the launch traced here: 367 us
  Pallas kernels  124 us (34%)
  waiting for transfers between devices  84.2 us (23%)
  blocking collectives  73.1 us (20%)
  starting transfers between devices  44.9 us (12%)
  local copies, waits for them, and re-layouts  17.8 us (5%)
  between operations  14.5 us (4%)
  other arithmetic  8.75 us (2%)
    pallas_call x2, Pallas kernels, expert_pass(): pl.pallas_call(functools.partial(expert_kernel, ff, cap, first, len(xdy))...  78.5 us
    reduce_scatter x1, waiting for transfers between devices, local_step(): lax.psum_scatter(grad_sum, ('z', 'y'), scatter_dimension=0, tiled=True)  42.3 us
    all_to_all x1, blocking collectives, local_step(): dg_back = lax.all_to_all(jnp.stack(dg_rows, axis=1), ring, 0, 0, tiled=True)  37 us
    ppermute x7, waiting for transfers between devices, local_step(): lax.ppermute(mine, ring, [(i, (i + k) % experts) for i in range(experts)])  36.2 us
    all_to_all x1, blocking collectives, local_step(): lax.all_to_all(dx_rows.reshape(experts, cap, d_model), ring, 0, 0, tiled=...  36.1 us
    pallas_call x1, Pallas kernels, combine(): pl.pallas_call(functools.partial(combine_kernel, owners, cap), grid=(micr...  20.3 us
    ppermute x7, starting transfers between devices, local_step(): lax.ppermute(block, ring, [(i, (i + k) % experts) for i in range(experts)])  19.2 us
    pallas_call x2, Pallas kernels, dispatch(): pl.pallas_call(functools.partial(dispatch_kernel, owners, cap), grid=(own...  19.2 us
  transfers between devices with their start and end apart: 24, of which 5 were waited for; matrix products, arithmetic and copies ran while one was open for 5% of the time, Pallas kernels for 23%

profile of v1, /device:TPU:0, one launch (start us, length us, event | category | flops | bytes accessed | tf_op | source)
XLA Modules:
  0.0 367.3 jit_solution(14509830553340353029)
XLA Ops:
  7.3 1.0 pad_maximum_fusion.1
  8.3 2.9 collective-permute-start.7
  13.0 2.0 collective-permute-done.7
  14.9 2.8 collective-permute-done.8
  17.7 0.9 collective-permute-done.9
  19.4 1.4 fusion.23
  20.8 1.3 pad_maximum_fusion.3
  22.2 1.4 collective-permute-start.2
  23.6 3.0 collective-permute-start.3
  27.2 9.6 %shard_map.110 = bf16[2560,1024]{1,0:T(8,128)(2,1)} custom-call(s32[2,2,1024]{2,1,0:T(2,128)} %get-tuple-element.22.own_ref, bf16[2,1024,512]{2,1,0:T(8,128)(2,1)} %x_ref.3, bf16[2,1024,512]{2,1,0:T(8,128)(2,1)} %dy_ref.3), custom_call_target="tpu_custom_call" | custom-call | flops 5368709120 | bytes 8388608 | tf_op jit(solution)/shard_map/pallas_call | solution.py:211
  36.8 4.6 %all-to-all-start = ((bf16[8,320,1024]{2,1,0:T(8,128)(2,1)}), bf16[8,320,1024]{2,1,0:T(8,128)(2,1)}, u32[]{:S(2)}, u32[]{:S(2)}) async-start(bf16[8,320,1024]{2,1,0:T(8,128)(2,1)} %bitcast.137), calls=%async_computation | async-start | bytes 10485760 | tf_op jit(solution)/shard_map/all_to_all | solution.py:382
  42.8 9.6 %shard_map.111 = bf16[2560,1024]{1,0:T(8,128)(2,1)} custom-call(s32[2,2,1024]{2,1,0:T(2,128)} %get-tuple-element.22.own_ref, bf16[2,1024,512]{2,1,0:T(8,128)(2,1)} %x_ref.3, bf16[2,1024,512]{2,1,0:T(8,128)(2,1)} %dy_ref.3), custom_call_target="tpu_custom_call" | custom-call | flops 5368709120 | bytes 8388608 | tf_op jit(solution)/shard_map/pallas_call | solution.py:211
  52.4 4.5 %dynamic-slice_bitcast_fusion = (bf16[320,1024]{1,0:T(8,128)(2,1)S(1)}, bf16[320,1024]{1,0:T(8,128)(2,1)S(1)}, bf16[320,1024]{1,0:T(8,128)(2,1)S(1)}, bf16[320,1...) fusion(bf16[8,320,1024]{2,1,0:T(8,128)(2,1)} %bitcast.138, ...), kind=kLoop, calls=%fused_computation.1 | loop fusion | bytes 10485792 | tf_op jit(solution)/shard_map/jit(dynamic_index_in_dim)/squeeze | solution.py:386
  56.9 3.0 collective-permute-start.5
  62.8 1.0 collective-permute-start.11
  66.0 36.1 %collective-permute-done.5 = f32[2,4,1024]{2,1,0:T(4,128)S(1)} collective-permute-done((f32[2,4,1024]{2,1,0:T(4,128)}, f32[2,4,1024]{2,1,0:T(4,128)S(1)}, u32[]{:S(2)}, u32[]{:S(2)}) %collective-permute-start.5) | collective-permute-done | bytes 32800 | tf_op jit(solution)/shard_map/ppermute | solution.py:348
  102.2 2.5 collective-permute-start.13
  106.5 6.1 %slot_gates.1 = f32[16,320]{1,0:T(8,128)} custom-call(s32[1]{0:T(128)} %bitcast.14.here_sm, f32[16,4,1024]{2,1,0:T(4,128)} %copy.19.table_ref), custom_call_target="tpu_custom_call" | custom-call | flops 10737418240 | bytes 1048576 | tf_op jit(solution)/shard_map/slot_gates/pallas_call | solution.py:248
  113.8 1.3 fusion.26
  115.9 0.9 collective-permute-start.15
  116.8 13.3 %collective-permute-start.16 = (bf16[320,1024]{1,0:T(8,128)(2,1)S(1)}, bf16[320,1024]{1,0:T(8,128)(2,1)}, u32[]{:S(2)}, u32[]{:S(2)}) collective-permute-start(bf16[320,1024]{1,0:T(8,128)(2,1)S(1)} %get-tuple-element.23), channel_id=1, source_target_pairs={{0,7},{1,0},{2,1},{3,2},{4,3},{5,4},{6,5},{7,6},{8,15},{9,8},{10,9... | collective-permute-start | bytes 1966088 | tf_op jit(solution)/shard_map/ppermute | solution.py:387
  130.7 38.9 %expert_first.1 = (bf16[2560,512]{1,0:T(8,128)(2,1)}, f32[8,320]{1,0:T(8,128)}, f32[512,5376]{1,0:T(8,128)}) custom-call(s32[8]{0:T(128)} %select_reduce_fusion.2.n_sm, s32[8]{0:T(128)} %iota.19.src_sm, bf16[2560,1024]{1,0:T(8,128)(2,1)} %bitcast.13.rest_0_, f32[8,320]{1,0:T(8,128)} %select_reduce_fusion.1.rest_1_, ...), custom_call_target="tpu_custom_call" | custom-call | flops 42278584320 | bytes 41943040 | tf_op jit(solution)/shard_map/expert_first/pallas_call | solution.py:169
  169.6 39.5 %expert_next.1 = (bf16[2560,512]{1,0:T(8,128)(2,1)}, f32[8,320]{1,0:T(8,128)}, f32[512,5376]{1,0:T(8,128)}) custom-call(s32[8]{0:T(128)} %get-tuple-element.51.n_sm, s32[8]{0:T(128)} %copy-done.7, bf16[320,1024]{1,0:T(8,128)(2,1)} %get-tuple-element.30.rest_0_, bf16[320,1024]{1,0:T(8,128)(2,1)} %collective-permute-done.10.rest_1_, ...), custom_call_target="tpu_custom_call" | custom-call | flops 42278584320 | bytes 41943040 | tf_op jit(solution)/shard_map/expert_next/pallas_call | solution.py:169
  210.1 37.0 %all_to_all.20 = f32[8,2,320]{2,1,0:T(2,128)S(1)} all-to-all(f32[8,2,320]{2,1,0:T(2,128)S(1)} %copy.20), channel_id=1, replica_groups=mesh['z'=4,'y'=4,'x'=4,'c'=2] {'x','c'}, dimensions={0} | all-to-all | bytes 40960 | tf_op jit(solution)/shard_map/all_to_all | solution.py:399
  247.0 36.1 %all_to_all.21 = bf16[8,320,512]{2,1,0:T(8,128)(2,1)} all-to-all(bf16[8,320,512]{2,1,0:T(8,128)(2,1)S(1)} %bitcast.141), channel_id=1, replica_groups=mesh['z'=4,'y'=4,'x'=4,'c'=2] {'x','c'}, dimensions={0} | all-to-all | bytes 5242880 | tf_op jit(solution)/shard_map/all_to_all | solution.py:396
  283.2 3.6 all-to-all-start.2
  288.2 42.3 %reduce-scatter.2.cloned.1.call-done = f32[32,5376]{1,0:T(8,128)} async-done(((f32[512,5376]{1,0:T(8,128)}), f32[32,5376]{1,0:T(8,128)}) %reduce-scatter.2.cloned.1.call-update) | async-done | bytes 688144 | tf_op jit(solution)/shard_map/reduce_scatter | solution.py:398
  330.5 1.8 dynamic-slice_bitcast_fusion.8
  332.3 2.7 collective-permute-start.17
  336.6 1.5 copy-done
  338.1 20.3 %combine.1 = (bf16[2,1024,512]{2,1,0:T(8,128)(2,1)}, f32[2,2,1024]{2,1,0:T(2,128)}) custom-call(s32[2,8]{1,0:T(2,128)} %broadcast_minimum_fusion.n_sm, s32[2,2,1024]{2,1,0:T(2,128)} %get-tuple-element.22.own_ref, f32[2,8,320]{2,1,0:T(8,128)} %bitcast.150, bf16[2560,512]{1,0:T(8,128)(2,1)} %bitcast.140, bf16[2560,512]{1,0:T(8,128)(2,1)} %bitcast.139), custom_call_target="tpu_custom_call" | custom-call | flops 5368709120 | bytes 12582912 | tf_op jit(solution)/shard_map/combine/pallas_call | solution.py:313
  358.5 1.0 fusion.2
  (82 shorter events, 18.5 us)
Async XLA Ops:
  7.2 123.0 %all-gather.2.cloned.1.call-start = ((), (), s32[]{:S(2)}) async-start(), calls=%async_computation.5 | async-start | bytes 5849088 | tf_op jit(solution)/shard_map/all_gather | solution.py:376
  8.3 6.6 %collective-permute-start.7 = (bf16[8,5376]{1,0:T(8,128)(2,1)S(1)}, bf16[8,5376]{1,0:T(8,128)(2,1)S(1)}, u32[]{:S(2)}, u32[]{:S(2)}) collective-permute-start(bf16[8,5376]{1,0:T(8,128)(2,1)S(1)} %get-tuple-element.47), channel_id=1, source_target_pairs={{0,6},{2,0},{4,2},{6,4},{1,7},{3,1},{5,3},{7,5},{8,14},{10,8},{12,... | collective-permute-start | bytes 258056 | tf_op jit(solution)/shard_map/ppermute | solution.py:365
  11.3 6.4 %collective-permute-start.8 = (bf16[8,5376]{1,0:T(8,128)(2,1)S(1)}, bf16[8,5376]{1,0:T(8,128)(2,1)S(1)}, u32[]{:S(2)}, u32[]{:S(2)}) collective-permute-start(bf16[8,5376]{1,0:T(8,128)(2,1)S(1)} %get-tuple-element.46), channel_id=1, source_target_pairs={{0,4},{2,6},{4,0},{6,2},{1,5},{3,7},{5,1},{7,3},{8,12},{10,14},{12... | collective-permute-start | bytes 258056 | tf_op jit(solution)/shard_map/ppermute | solution.py:365
  12.1 6.5 %collective-permute-start.9 = (bf16[8,5376]{1,0:T(8,128)(2,1)S(1)}, bf16[8,5376]{1,0:T(8,128)(2,1)S(1)}, u32[]{:S(2)}, u32[]{:S(2)}) collective-permute-start(bf16[8,5376]{1,0:T(8,128)(2,1)S(1)} %get-tuple-element.45), channel_id=1, source_target_pairs={{0,2},{2,4},{4,6},{6,0},{1,3},{3,5},{5,7},{7,1},{8,10},{10,12},{12... | collective-permute-start | bytes 258056 | tf_op jit(solution)/shard_map/ppermute | solution.py:365
  22.2 34.7 %collective-permute-start = (f32[2,4,1024]{2,1,0:T(4,128)}, f32[2,4,1024]{2,1,0:T(4,128)}, u32[]{:S(2)}, u32[]{:S(2)}) collective-permute-start(f32[2,4,1024]{2,1,0:T(4,128)} %pad_maximum_fusion.3), channel_id=1, source_target_pairs={{0,1},{1,2},{2,3},{3,4},{4,5},{5,6},{6,7},{7,0},{8,9},{9,10},{10,1... | collective-permute-start | bytes 98312 | tf_op jit(solution)/shard_map/ppermute | solution.py:348
  22.2 38.5 %collective-permute-start.1 = (f32[2,4,1024]{2,1,0:T(4,128)}, f32[2,4,1024]{2,1,0:T(4,128)}, u32[]{:S(2)}, u32[]{:S(2)}) collective-permute-start(f32[2,4,1024]{2,1,0:T(4,128)} %pad_maximum_fusion.3), channel_id=1, source_target_pairs={{0,2},{1,3},{2,4},{3,5},{4,6},{5,7},{6,0},{7,1},{8,10},{9,11},{10,... | collective-permute-start | bytes 98312 | tf_op jit(solution)/shard_map/ppermute | solution.py:348
  22.2 39.6 %collective-permute-start.2 = (f32[2,4,1024]{2,1,0:T(4,128)}, f32[2,4,1024]{2,1,0:T(4,128)}, u32[]{:S(2)}, u32[]{:S(2)}) collective-permute-start(f32[2,4,1024]{2,1,0:T(4,128)} %pad_maximum_fusion.3), channel_id=1, source_target_pairs={{0,3},{1,4},{2,5},{3,6},{4,7},{5,0},{6,1},{7,2},{8,11},{9,12},{10,... | collective-permute-start | bytes 98312 | tf_op jit(solution)/shard_map/ppermute | solution.py:348
  23.6 39.2 %collective-permute-start.3 = (f32[2,4,1024]{2,1,0:T(4,128)}, f32[2,4,1024]{2,1,0:T(4,128)}, u32[]{:S(2)}, u32[]{:S(2)}) collective-permute-start(f32[2,4,1024]{2,1,0:T(4,128)} %pad_maximum_fusion.3), channel_id=1, source_target_pairs={{0,4},{1,5},{2,6},{3,7},{4,0},{5,1},{6,2},{7,3},{8,12},{9,13},{10,... | collective-permute-start | bytes 98312 | tf_op jit(solution)/shard_map/ppermute | solution.py:348
  26.6 38.0 %collective-permute-start.4 = (f32[2,4,1024]{2,1,0:T(4,128)}, f32[2,4,1024]{2,1,0:T(4,128)}, u32[]{:S(2)}, u32[]{:S(2)}) collective-permute-start(f32[2,4,1024]{2,1,0:T(4,128)} %pad_maximum_fusion.3), channel_id=1, source_target_pairs={{0,5},{1,6},{2,7},{3,0},{4,1},{5,2},{6,3},{7,4},{8,13},{9,14},{10,... | collective-permute-start | bytes 98312 | tf_op jit(solution)/shard_map/ppermute | solution.py:348
  36.8 93.4 %all-to-all-start = ((bf16[8,320,1024]{2,1,0:T(8,128)(2,1)}), bf16[8,320,1024]{2,1,0:T(8,128)(2,1)}, u32[]{:S(2)}, u32[]{:S(2)}) async-start(bf16[8,320,1024]{2,1,0:T(8,128)(2,1)} %bitcast.137), calls=%async_computation | async-start | bytes 10485760 | tf_op jit(solution)/shard_map/all_to_all | solution.py:382
  41.4 289.1 %reduce-scatter.2.cloned.1.call-start = ((), (), s32[]{:S(2)}) async-start(), calls=%async_computation.6 | async-start | bytes 11698176 | tf_op jit(solution)/shard_map/reduce_scatter | solution.py:398
  52.4 4.5 %copy-start.3 = (f32[2,1024,2]{1,2,0:T(2,128)S(1)}, f32[2,1024,2]{1,2,0:T(2,128)}, u32[]{:S(2)}) copy-start(f32[2,1024,2]{1,2,0:T(2,128)} %param.10) | copy-start | bytes 49156
  56.9 45.2 %collective-permute-start.5 = (f32[2,4,1024]{2,1,0:T(4,128)}, f32[2,4,1024]{2,1,0:T(4,128)S(1)}, u32[]{:S(2)}, u32[]{:S(2)}) collective-permute-start(f32[2,4,1024]{2,1,0:T(4,128)} %pad_maximum_fusion.3), channel_id=1, source_target_pairs={{0,6},{1,7},{2,0},{3,1},{4,2},{5,3},{6,4},{7,5},{8,14},{9,15},{10,... | collective-permute-start | bytes 98312 | tf_op jit(solution)/shard_map/ppermute | solution.py:348
  60.7 44.0 %collective-permute-start.6 = (f32[2,4,1024]{2,1,0:T(4,128)}, f32[2,4,1024]{2,1,0:T(4,128)S(1)}, u32[]{:S(2)}, u32[]{:S(2)}) collective-permute-start(f32[2,4,1024]{2,1,0:T(4,128)} %pad_maximum_fusion.3), channel_id=1, source_target_pairs={{0,7},{1,0},{2,1},{3,2},{4,3},{5,4},{6,5},{7,6},{8,15},{9,8},{10,9... | collective-permute-start | bytes 98312 | tf_op jit(solution)/shard_map/ppermute | solution.py:348
  61.8 54.1 %collective-permute-start.10 = (bf16[320,1024]{1,0:T(8,128)(2,1)}, bf16[320,1024]{1,0:T(8,128)(2,1)}, u32[]{:S(2)}, u32[]{:S(2)}) collective-permute-start(bf16[320,1024]{1,0:T(8,128)(2,1)} %get-tuple-element.29), channel_id=1, source_target_pairs={{0,1},{1,2},{2,3},{3,4},{4,5},{5,6},{6,7},{7,0},{8,9},{9,10},{10,1... | collective-permute-start | bytes 1966088 | tf_op jit(solution)/shard_map/ppermute | solution.py:387
  62.8 54.0 %collective-permute-start.11 = (bf16[320,1024]{1,0:T(8,128)(2,1)}, bf16[320,1024]{1,0:T(8,128)(2,1)}, u32[]{:S(2)}, u32[]{:S(2)}) collective-permute-start(bf16[320,1024]{1,0:T(8,128)(2,1)} %get-tuple-element.28), channel_id=1, source_target_pairs={{0,2},{1,3},{2,4},{3,5},{4,6},{5,7},{6,0},{7,1},{8,10},{9,11},{10,... | collective-permute-start | bytes 1966088 | tf_op jit(solution)/shard_map/ppermute | solution.py:387
  64.6 105.0 %collective-permute-start.12 = (bf16[320,1024]{1,0:T(8,128)(2,1)S(1)}, bf16[320,1024]{1,0:T(8,128)(2,1)}, u32[]{:S(2)}, u32[]{:S(2)}) collective-permute-start(bf16[320,1024]{1,0:T(8,128)(2,1)S(1)} %get-tuple-element.27), channel_id=1, source_target_pairs={{0,3},{1,4},{2,5},{3,6},{4,7},{5,0},{6,1},{7,2},{8,11},{9,12},{10,... | collective-permute-start | bytes 1966088 | tf_op jit(solution)/shard_map/ppermute | solution.py:387
  102.2 67.4 %collective-permute-start.13 = (bf16[320,1024]{1,0:T(8,128)(2,1)S(1)}, bf16[320,1024]{1,0:T(8,128)(2,1)}, u32[]{:S(2)}, u32[]{:S(2)}) collective-permute-start(bf16[320,1024]{1,0:T(8,128)(2,1)S(1)} %get-tuple-element.26), channel_id=1, source_target_pairs={{0,4},{1,5},{2,6},{3,7},{4,0},{5,1},{6,2},{7,3},{8,12},{9,13},{10,... | collective-permute-start | bytes 1966088 | tf_op jit(solution)/shard_map/ppermute | solution.py:387
  104.7 64.9 %collective-permute-start.14 = (bf16[320,1024]{1,0:T(8,128)(2,1)S(1)}, bf16[320,1024]{1,0:T(8,128)(2,1)}, u32[]{:S(2)}, u32[]{:S(2)}) collective-permute-start(bf16[320,1024]{1,0:T(8,128)(2,1)S(1)} %get-tuple-element.25), channel_id=1, source_target_pairs={{0,5},{1,6},{2,7},{3,0},{4,1},{5,2},{6,3},{7,4},{8,13},{9,14},{10,... | collective-permute-start | bytes 1966088 | tf_op jit(solution)/shard_map/ppermute | solution.py:387
  106.5 6.6 %copy-start.8 = (s32[8]{0:T(128)S(1)}, s32[8]{0:T(128)}, u32[]{:S(2)}) copy-start(s32[8]{0:T(128)} %copy-done.7) | copy-start | bytes 100
  106.5 8.7 %copy-start.6 = (pred[8,8]{1,0:T(8,128)(4,1)S(1)}, pred[8,8]{1,0:T(8,128)(4,1)}, u32[]{:S(2)}) copy-start(pred[8,8]{1,0:T(8,128)(4,1)} %iota_compare_fusion.1) | copy-start | bytes 196
  115.9 53.7 %collective-permute-start.15 = (bf16[320,1024]{1,0:T(8,128)(2,1)S(1)}, bf16[320,1024]{1,0:T(8,128)(2,1)}, u32[]{:S(2)}, u32[]{:S(2)}) collective-permute-start(bf16[320,1024]{1,0:T(8,128)(2,1)S(1)} %get-tuple-element.24), channel_id=1, source_target_pairs={{0,6},{1,7},{2,0},{3,1},{4,2},{5,3},{6,4},{7,5},{8,14},{9,15},{10,... | collective-permute-start | bytes 1966088 | tf_op jit(solution)/shard_map/ppermute | solution.py:387
  116.8 52.8 %collective-permute-start.16 = (bf16[320,1024]{1,0:T(8,128)(2,1)S(1)}, bf16[320,1024]{1,0:T(8,128)(2,1)}, u32[]{:S(2)}, u32[]{:S(2)}) collective-permute-start(bf16[320,1024]{1,0:T(8,128)(2,1)S(1)} %get-tuple-element.23), channel_id=1, source_target_pairs={{0,7},{1,0},{2,1},{3,2},{4,3},{5,4},{6,5},{7,6},{8,15},{9,8},{10,9... | collective-permute-start | bytes 1966088 | tf_op jit(solution)/shard_map/ppermute | solution.py:387
  209.2 0.7 copy-start.4
  209.2 0.8 copy-start.5
  209.2 37.8 %copy-start.1 = (bf16[2560,512]{1,0:T(8,128)(2,1)S(1)}, bf16[2560,512]{1,0:T(8,128)(2,1)}, u32[]{:S(2)}) copy-start(bf16[2560,512]{1,0:T(8,128)(2,1)} %get-tuple-element.17) | copy-start | bytes 7864324
  247.0 39.8 %copy-start.2 = (s32[2,2,1024]{2,1,0:T(2,128)S(1)}, s32[2,2,1024]{2,1,0:T(2,128)}, u32[]{:S(2)}) copy-start(s32[2,2,1024]{2,1,0:T(2,128)} %get-tuple-element.22.own_ref) | copy-start | bytes 49156
  283.2 53.5 %all-to-all-start.2 = ((bf16[8,320,512]{2,1,0:T(8,128)(2,1)}), bf16[8,320,512]{2,1,0:T(8,128)(2,1)S(1)}, u32[]{:S(2)}, u32[]{:S(2)}) async-start(bf16[8,320,512]{2,1,0:T(8,128)(2,1)} %bitcast.33), calls=%async_computation.2 | async-start | bytes 5242880 | tf_op jit(solution)/shard_map/all_to_all | solution.py:396
  332.3 26.2 %collective-permute-start.17 = (f32[8,5376]{1,0:T(8,128)}, f32[8,5376]{1,0:T(8,128)S(1)}, u32[]{:S(2)}, u32[]{:S(2)}) collective-permute-start(f32[8,5376]{1,0:T(8,128)} %get-tuple-element.40), channel_id=1, source_target_pairs={{0,6},{2,0},{4,2},{6,4},{1,7},{3,1},{5,3},{7,5},{8,14},{10,8},{12,... | collective-permute-start | bytes 516104 | tf_op jit(solution)/shard_map/ppermute | solution.py:365
  335.0 23.5 %collective-permute-start.18 = (f32[8,5376]{1,0:T(8,128)S(1)}, f32[8,5376]{1,0:T(8,128)S(1)}, u32[]{:S(2)}, u32[]{:S(2)}) collective-permute-start(f32[8,5376]{1,0:T(8,128)S(1)} %get-tuple-element.39), channel_id=1, source_target_pairs={{0,4},{2,6},{4,0},{6,2},{1,5},{3,7},{5,1},{7,3},{8,12},{10,14},{12... | collective-permute-start | bytes 516104 | tf_op jit(solution)/shard_map/ppermute | solution.py:365
  335.8 22.7 %collective-permute-start.19 = (f32[8,5376]{1,0:T(8,128)S(1)}, f32[8,5376]{1,0:T(8,128)S(1)}, u32[]{:S(2)}, u32[]{:S(2)}) collective-permute-start(f32[8,5376]{1,0:T(8,128)S(1)} %get-tuple-element.38), channel_id=1, source_target_pairs={{0,2},{2,4},{4,6},{6,0},{1,3},{3,5},{5,7},{7,1},{8,10},{10,12},{12... | collective-permute-start | bytes 516104 | tf_op jit(solution)/shard_map/ppermute | solution.py:365
  336.6 1.5 copy-start
  (1 other events, 0.5 us)
Sparse Core Ops, SparseCore 0:
  19.6 57.7 all-gather.1
  209.4 121.0 reduce-scatter.1
